TPU v7x, 32 devices: a whole 2x2x4 slice. The times are simulated.
32 devices in a mesh: site: 2 (over core), rows: 2 (over x), cols: 8 (over z, y).
Axes of the slice: x: 2, y: 2, z: 4, core: 2. Of those that a mesh axis runs over, the one named last changes fastest.
Arguments:
- tracer: float32 [128, 256, 128], P(('site', 'rows'), 'cols'), parts along dimension 0, may hold values from 0.5 to 2
- flow_y: float32 [128, 256, 128], P(('site', 'rows'), 'cols'), parts along dimension 0, may hold values from -0.3 to 0.3
- flow_x: float32 [128, 256, 128], P(('site', 'rows'), 'cols'), parts along dimension 0, may hold values from -0.3 to 0.3
Outputs:
- scaled_field: float32 [128, 256, 128], P(('site', 'rows'), 'cols'), parts along dimension 0
- tracer_end: float32 [128, 256, 128], P(('site', 'rows'), 'cols'), parts along dimension 0
There are 2 independent parts, one for each index of `site`. A program takes and returns all parts, laid end to end along the dimension named above; each array names one. Nothing has to cross between parts.
All inputs are finite; a program needn't handle non-finite values.
Results may differ from a plain program's by a relative error of at most 0.00002.
Values sent between devices are 32-bit elements; how exact they have to be, the bound alone decides.
A program may use at most 64 MiB of HBM per device.

v0:
```python
import jax
import jax.numpy as jnp
from jax import lax
from jax.sharding import PartitionSpec as P

STEPS = 6


def with_halo(block, sides, width):
    for axis, dim in sides:
        count = lax.axis_size(axis)
        forward = [(i, i + 1) for i in range(count - 1)]
        backward = [(target, source) for source, target in forward]
        low = lax.ppermute(
            lax.slice_in_dim(block, block.shape[dim] - width, None, axis=dim), axis, forward
        )
        high = lax.ppermute(lax.slice_in_dim(block, 0, width, axis=dim), axis, backward)
        block = jnp.concatenate([low, block, high], axis=dim)
    return block


def strip_edges(values, dims):
    for dim in dims:
        values = lax.slice_in_dim(values, 1, values.shape[dim] - 1, axis=dim)
    return values


def neighbour(values, dim, start, dims):
    others = [other for other in dims if other != dim]
    values = strip_edges(values, others)
    return lax.slice_in_dim(values, start, start + values.shape[dim] - 2, axis=dim)


def one_step(padded, flow_y, flow_x):
    middle = strip_edges(padded, (0, 1))
    lower = [neighbour(padded, dim, 0, (0, 1)) for dim in (0, 1)]
    upper = [neighbour(padded, dim, 2, (0, 1)) for dim in (0, 1)]
    slopes = [above - below for above, below in zip(upper, lower)]
    smooth_rate = 0.05
    spread = lower[0] + upper[0] + lower[1] + upper[1] - 4.0 * middle
    return middle - flow_y * slopes[0] - flow_x * slopes[1] + smooth_rate * spread


def shards(tracer, flow_y, flow_x):
    padded = with_halo(tracer, (("rows", 0), ("cols", 1)), STEPS)
    wide_parts = with_halo(
        jnp.concatenate([flow_y, flow_x], axis=2), (("rows", 0), ("cols", 1)), STEPS - 1
    )
    wide_flow_y, wide_flow_x = jnp.split(wide_parts, 2, axis=2)
    for step in range(STEPS):
        later = one_step(padded, wide_flow_y, wide_flow_x)
        values = later
        margin = STEPS - 1 - step
        place = lax.axis_index("rows") * tracer.shape[0] - margin + jnp.arange(values.shape[0])
        keep_cells = (place >= 0) & (place < tracer.shape[0] * lax.axis_size("rows"))
        values = jnp.where(keep_cells.reshape((-1,) + (1,) * 2), values, 0.0)
        place = lax.axis_index("cols") * tracer.shape[1] - margin + jnp.arange(values.shape[1])
        keep_cells = (place >= 0) & (place < tracer.shape[1] * lax.axis_size("cols"))
        values = jnp.where(keep_cells.reshape((-1,) + (1,) * 1), values, 0.0)
        later = values
        if step < STEPS - 1:
            wide_flow_y = strip_edges(wide_flow_y, (0, 1))
            wide_flow_x = strip_edges(wide_flow_x, (0, 1))
        padded = later
    tracer = padded
    count = tracer.shape[1] * lax.axis_size("cols")
    line_mean = lax.psum(jnp.sum(tracer, axis=1, keepdims=True), "cols") / count
    centred = tracer - line_mean
    line_variance = lax.psum(jnp.sum(centred * centred, axis=1, keepdims=True), "cols") / count
    scaled_field = centred * lax.rsqrt(line_variance + 0.0001)
    return (scaled_field, tracer)


def solution(mesh):
    placed = (
        P(("site", "rows"), "cols", None),
        P(("site", "rows"), "cols", None),
        P(("site", "rows"), "cols", None),
    )
    return jax.shard_map(
        shards,
        mesh=mesh,
        in_specs=placed,
        out_specs=(P(("site", "rows"), "cols", None), P(("site", "rows"), "cols", None)),
        check_vma=False,
    )
```

profile of v0, /device:TPU:0, one launch (start us, length us, event | category | flops | bytes accessed | tf_op | source)
XLA Modules:
  0.0 118.2 jit_solution(12935448793443510609)
XLA Ops:
  0.6 1.1 constant_dynamic-update-slice_fusion.4
  1.8 1.1 constant_dynamic-update-slice_fusion.3
  2.9 1.3 %collective-permute-start.5 = (f32[5,32,256]{2,1,0:T(8,128)S(1)}, f32[5,32,256]{2,1,0:T(8,128)S(1)}, u32[]{:S(2)}, u32[]{:S(2)}) collective-permute-start(f32[5,32,256]{2,1,0:T(8,128)S(1)} %get-tuple-element.7), channel_id=1, source_target_pairs={{8,0},{9,1},{10,2},{11,3},{12,4},{13,5},{14,6},{15,7},{24,16},{25,... | collective-permute-start | bytes 491528 | tf_op jit(solution)/shard_map/ppermute | solution.py:17
  4.2 4.9 %collective-permute-start.4 = (f32[5,32,256]{2,1,0:T(8,128)S(1)}, f32[5,32,256]{2,1,0:T(8,128)S(1)}, u32[]{:S(2)}, u32[]{:S(2)}) collective-permute-start(f32[5,32,256]{2,1,0:T(8,128)S(1)} %get-tuple-element.6), channel_id=1, source_target_pairs={{0,8},{1,9},{2,10},{3,11},{4,12},{5,13},{6,14},{7,15},{16,24},{17,... | collective-permute-start | bytes 491528 | tf_op jit(solution)/shard_map/ppermute | solution.py:14
  9.1 1.3 %collective-permute-start = (f32[6,32,128]{2,1,0:T(8,128)S(1)}, f32[6,32,128]{2,1,0:T(8,128)S(1)}, u32[]{:S(2)}, u32[]{:S(2)}) collective-permute-start(f32[6,32,128]{2,1,0:T(8,128)S(1)} %get-tuple-element.11), channel_id=1, source_target_pairs={{0,8},{1,9},{2,10},{3,11},{4,12},{5,13},{6,14},{7,15},{16,24},{17,... | collective-permute-start | bytes 294920 | tf_op jit(solution)/shard_map/ppermute | solution.py:14
  10.4 1.3 %collective-permute-start.1 = (f32[6,32,128]{2,1,0:T(8,128)S(1)}, f32[6,32,128]{2,1,0:T(8,128)S(1)}, u32[]{:S(2)}, u32[]{:S(2)}) collective-permute-start(f32[6,32,128]{2,1,0:T(8,128)S(1)} %get-tuple-element.10), channel_id=1, source_target_pairs={{8,0},{9,1},{10,2},{11,3},{12,4},{13,5},{14,6},{15,7},{24,16},{25,... | collective-permute-start | bytes 294920 | tf_op jit(solution)/shard_map/ppermute | solution.py:17
  11.8 2.9 %collective-permute-done = f32[6,32,128]{2,1,0:T(8,128)S(1)} collective-permute-done((f32[6,32,128]{2,1,0:T(8,128)S(1)}, f32[6,32,128]{2,1,0:T(8,128)S(1)}, u32[]{:S(2)}, u32[]{:S(2)}) %collective-permute-start) | collective-permute-done | bytes 98336 | tf_op jit(solution)/shard_map/ppermute | solution.py:14
  14.7 2.2 %collective-permute-done.1 = f32[6,32,128]{2,1,0:T(8,128)S(1)} collective-permute-done((f32[6,32,128]{2,1,0:T(8,128)S(1)}, f32[6,32,128]{2,1,0:T(8,128)S(1)}, u32[]{:S(2)}, u32[]{:S(2)}) %collective-permute-start.1) | collective-permute-done | bytes 98336 | tf_op jit(solution)/shard_map/ppermute | solution.py:17
  17.0 1.3 %collective-permute-start.3 = (f32[44,6,128]{2,1,0:T(8,128)S(1)}, f32[44,6,128]{2,1,0:T(8,128)S(1)}, u32[]{:S(2)}, u32[]{:S(2)}) collective-permute-start(f32[44,6,128]{2,1,0:T(8,128)S(1)} %get-tuple-element.9), channel_id=1, source_target_pairs={{1,0},{2,1},{3,2},{4,3},{5,4},{6,5},{7,6},{9,8},{10,9},{11,10},{12... | collective-permute-start | bytes 405512 | tf_op jit(solution)/shard_map/ppermute | solution.py:17
  18.3 5.2 %collective-permute-start.2 = (f32[44,6,128]{2,1,0:T(8,128)S(1)}, f32[44,6,128]{2,1,0:T(8,128)S(1)}, u32[]{:S(2)}, u32[]{:S(2)}) collective-permute-start(f32[44,6,128]{2,1,0:T(8,128)S(1)} %get-tuple-element.8), channel_id=1, source_target_pairs={{0,1},{1,2},{2,3},{3,4},{4,5},{5,6},{6,7},{8,9},{9,10},{10,11},{11... | collective-permute-start | bytes 405512 | tf_op jit(solution)/shard_map/ppermute | solution.py:14
  23.5 0.1 pad_maximum_fusion.4
  23.6 1.3 %collective-permute-start.7 = (f32[42,5,256]{2,1,0:T(8,128)S(1)}, f32[42,5,256]{2,1,0:T(8,128)S(1)}, u32[]{:S(2)}, u32[]{:S(2)}) collective-permute-start(f32[42,5,256]{2,1,0:T(8,128)S(1)} %get-tuple-element.5), channel_id=1, source_target_pairs={{1,0},{2,1},{3,2},{4,3},{5,4},{6,5},{7,6},{9,8},{10,9},{11,10},{12... | collective-permute-start | bytes 645128 | tf_op jit(solution)/shard_map/ppermute | solution.py:17
  24.9 5.5 %collective-permute-start.6 = (f32[42,5,256]{2,1,0:T(8,128)S(1)}, f32[42,5,256]{2,1,0:T(8,128)S(1)}, u32[]{:S(2)}, u32[]{:S(2)}) collective-permute-start(f32[42,5,256]{2,1,0:T(8,128)S(1)} %get-tuple-element.4), channel_id=1, source_target_pairs={{0,1},{1,2},{2,3},{3,4},{4,5},{5,6},{6,7},{8,9},{9,10},{10,11},{11... | collective-permute-start | bytes 645128 | tf_op jit(solution)/shard_map/ppermute | solution.py:14
  30.4 6.4 %collective-permute-done.2 = f32[44,6,128]{2,1,0:T(8,128)S(1)} collective-permute-done((f32[44,6,128]{2,1,0:T(8,128)S(1)}, f32[44,6,128]{2,1,0:T(8,128)S(1)}, u32[]{:S(2)}, u32[]{:S(2)}) %collective-permute-start.2) | collective-permute-done | bytes 135200 | tf_op jit(solution)/shard_map/ppermute | solution.py:14
  36.8 0.1 pad_maximum_fusion.1
  36.9 6.2 %collective-permute-done.6 = f32[42,5,256]{2,1,0:T(8,128)S(1)} collective-permute-done((f32[42,5,256]{2,1,0:T(8,128)S(1)}, f32[42,5,256]{2,1,0:T(8,128)S(1)}, u32[]{:S(2)}, u32[]{:S(2)}) %collective-permute-start.6) | collective-permute-done | bytes 215072 | tf_op jit(solution)/shard_map/ppermute | solution.py:14
  43.2 0.3 pad_maximum_fusion
  43.5 0.7 fusion.3
  44.2 0.6 fusion.8
  44.8 0.7 fusion.13
  45.5 0.6 fusion.18
  46.1 0.0 copy-start.1
  46.1 0.0 copy-start.2
  46.1 0.6 fusion.23
  46.7 0.4 copy-done.1
  47.2 0.2 copy-done.2
  47.3 0.4 fusion.25
  47.8 0.0 copy-start
  47.8 36.4 %psum.14 = f32[32,1,128]{2,0,1:T(8,128)S(1)} all-reduce(f32[32,1,128]{2,0,1:T(8,128)S(1)} %bitcast.6), channel_id=1, replica_groups=mesh['site'=2,'rows'=2,'cols'=8] {'cols'}, use_global_device_ids=true, to_apply=%region_1.2 | all-reduce | flops 4096 | bytes 32768 | tf_op jit(solution)/shard_map/psum | solution.py:67
  84.2 0.1 multiply_reduce_fusion
  84.3 33.0 %psum.15 = f32[32,1,128]{2,0,1:T(8,128)S(1)} all-reduce(f32[32,1,128]{2,0,1:T(8,128)S(1)} %bitcast.7), channel_id=1, replica_groups=mesh['site'=2,'rows'=2,'cols'=8] {'cols'}, use_global_device_ids=true, to_apply=%region_3.4 | all-reduce | flops 4096 | bytes 32768 | tf_op jit(solution)/shard_map/psum | solution.py:69
  117.3 0.9 subtract_multiply_fusion
  (21 shorter events, 0.2 us)
Async XLA Ops:
  0.6 8.5 %copy-start.3 = (f32[32,32,128]{2,1,0:T(8,128)S(1)}, f32[32,32,128]{2,1,0:T(8,128)}, u32[]{:S(2)}) copy-start(f32[32,32,128]{2,1,0:T(8,128)} %param.3) | copy-start | bytes 1572868
  2.9 20.6 %collective-permute-start.5 = (f32[5,32,256]{2,1,0:T(8,128)S(1)}, f32[5,32,256]{2,1,0:T(8,128)S(1)}, u32[]{:S(2)}, u32[]{:S(2)}) collective-permute-start(f32[5,32,256]{2,1,0:T(8,128)S(1)} %get-tuple-element.7), channel_id=1, source_target_pairs={{8,0},{9,1},{10,2},{11,3},{12,4},{13,5},{14,6},{15,7},{24,16},{25,... | collective-permute-start | bytes 491528 | tf_op jit(solution)/shard_map/ppermute | solution.py:17
  4.2 19.3 %collective-permute-start.4 = (f32[5,32,256]{2,1,0:T(8,128)S(1)}, f32[5,32,256]{2,1,0:T(8,128)S(1)}, u32[]{:S(2)}, u32[]{:S(2)}) collective-permute-start(f32[5,32,256]{2,1,0:T(8,128)S(1)} %get-tuple-element.6), channel_id=1, source_target_pairs={{0,8},{1,9},{2,10},{3,11},{4,12},{5,13},{6,14},{7,15},{16,24},{17,... | collective-permute-start | bytes 491528 | tf_op jit(solution)/shard_map/ppermute | solution.py:14
  9.1 5.6 %collective-permute-start = (f32[6,32,128]{2,1,0:T(8,128)S(1)}, f32[6,32,128]{2,1,0:T(8,128)S(1)}, u32[]{:S(2)}, u32[]{:S(2)}) collective-permute-start(f32[6,32,128]{2,1,0:T(8,128)S(1)} %get-tuple-element.11), channel_id=1, source_target_pairs={{0,8},{1,9},{2,10},{3,11},{4,12},{5,13},{6,14},{7,15},{16,24},{17,... | collective-permute-start | bytes 294920 | tf_op jit(solution)/shard_map/ppermute | solution.py:14
  10.4 6.5 %collective-permute-start.1 = (f32[6,32,128]{2,1,0:T(8,128)S(1)}, f32[6,32,128]{2,1,0:T(8,128)S(1)}, u32[]{:S(2)}, u32[]{:S(2)}) collective-permute-start(f32[6,32,128]{2,1,0:T(8,128)S(1)} %get-tuple-element.10), channel_id=1, source_target_pairs={{8,0},{9,1},{10,2},{11,3},{12,4},{13,5},{14,6},{15,7},{24,16},{25,... | collective-permute-start | bytes 294920 | tf_op jit(solution)/shard_map/ppermute | solution.py:17
  17.0 13.4 %collective-permute-start.3 = (f32[44,6,128]{2,1,0:T(8,128)S(1)}, f32[44,6,128]{2,1,0:T(8,128)S(1)}, u32[]{:S(2)}, u32[]{:S(2)}) collective-permute-start(f32[44,6,128]{2,1,0:T(8,128)S(1)} %get-tuple-element.9), channel_id=1, source_target_pairs={{1,0},{2,1},{3,2},{4,3},{5,4},{6,5},{7,6},{9,8},{10,9},{11,10},{12... | collective-permute-start | bytes 405512 | tf_op jit(solution)/shard_map/ppermute | solution.py:17
  18.3 18.5 %collective-permute-start.2 = (f32[44,6,128]{2,1,0:T(8,128)S(1)}, f32[44,6,128]{2,1,0:T(8,128)S(1)}, u32[]{:S(2)}, u32[]{:S(2)}) collective-permute-start(f32[44,6,128]{2,1,0:T(8,128)S(1)} %get-tuple-element.8), channel_id=1, source_target_pairs={{0,1},{1,2},{2,3},{3,4},{4,5},{5,6},{6,7},{8,9},{9,10},{10,11},{11... | collective-permute-start | bytes 405512 | tf_op jit(solution)/shard_map/ppermute | solution.py:14
  23.6 13.3 %collective-permute-start.7 = (f32[42,5,256]{2,1,0:T(8,128)S(1)}, f32[42,5,256]{2,1,0:T(8,128)S(1)}, u32[]{:S(2)}, u32[]{:S(2)}) collective-permute-start(f32[42,5,256]{2,1,0:T(8,128)S(1)} %get-tuple-element.5), channel_id=1, source_target_pairs={{1,0},{2,1},{3,2},{4,3},{5,4},{6,5},{7,6},{9,8},{10,9},{11,10},{12... | collective-permute-start | bytes 645128 | tf_op jit(solution)/shard_map/ppermute | solution.py:17
  24.9 18.3 %collective-permute-start.6 = (f32[42,5,256]{2,1,0:T(8,128)S(1)}, f32[42,5,256]{2,1,0:T(8,128)S(1)}, u32[]{:S(2)}, u32[]{:S(2)}) collective-permute-start(f32[42,5,256]{2,1,0:T(8,128)S(1)} %get-tuple-element.4), channel_id=1, source_target_pairs={{0,1},{1,2},{2,3},{3,4},{4,5},{5,6},{6,7},{8,9},{9,10},{10,11},{11... | collective-permute-start | bytes 645128 | tf_op jit(solution)/shard_map/ppermute | solution.py:14
  46.1 1.0 copy-start.1
  46.1 1.2 %copy-start.2 = (f32[32,32,128]{2,1,0:T(8,128)S(1)}, f32[32,32,128]{2,1,0:T(8,128)}, u32[]{:S(2)}) copy-start(f32[32,32,128]{2,1,0:T(8,128)} %param.4) | copy-start | bytes 1572868
  47.8 70.4 %copy-start = (f32[32,32,128]{2,1,0:T(8,128)}, f32[32,32,128]{2,1,0:T(8,128)S(1)}, u32[]{:S(2)}) copy-start(f32[32,32,128]{2,1,0:T(8,128)S(1)} %get-tuple-element.3) | copy-start | bytes 1572868
where the time goes:
time: 119 us; the launch traced here: 118 us
  blocking collectives  69.4 us (58%)
  starting transfers between devices  22 us (18%)
  waiting for transfers between devices  17.7 us (15%)
  other arithmetic  5.2 us (4%)
  local copies, waits for them, and re-layouts  2.94 us (2%)
    psum x1, blocking collectives, shards(): line_mean = lax.psum(jnp.sum(tracer, axis=1, keepdims=True), 'cols') / count  36.4 us
    psum x1, blocking collectives, shards(): lax.psum(jnp.sum(centred * centred, axis=1, keepdims=True), 'cols') / count  33 us
    ppermute x4, starting transfers between devices, with_halo(): lax.ppermute(lax.slice_in_dim(block, block.shape[dim] - width, None, axis...  16.9 us
    ppermute x4, waiting for transfers between devices, with_halo(): lax.ppermute(lax.slice_in_dim(block, block.shape[dim] - width, None, axis...  15.5 us
    ppermute x4, starting transfers between devices, with_halo(): lax.ppermute(lax.slice_in_dim(block, 0, width, axis=dim), axis, backward)  5.17 us
    select_n x5, other arithmetic, shards(): values = jnp.where(keep_cells.reshape((-1,) + (1,) * 1), values, 0.0)  3.2 us
  transfers between devices with their start and end apart: 8, of which 4 were waited for; matrix products, arithmetic and copies ran while one was open for 0% of the time, Pallas kernels for 0%

commit v1 on v0

v1 whole, which is shorter than its diff:
```python
import functools

import jax
import jax.numpy as jnp
from jax import lax
from jax.experimental import pallas as pl
from jax.experimental.pallas import tpu as pltpu
from jax.sharding import PartitionSpec as P

MESH = pl.DeviceIdType.MESH
DEPTHS = (3, 3)
PAD = 8
SIDES = tuple((dy, dx) for dy in (-1, 0, 1) for dx in (-1, 0, 1) if (dy, dx) != (0, 0))


def spans(side, depth, size, first):
    if side == 0:
        return pl.ds(0, size), pl.ds(first, size)
    if side < 0:
        return pl.ds(0, depth), pl.ds(first + size, depth)
    return pl.ds(size - depth, depth), pl.ds(first - depth, depth)


def kernel(rows, cols, by, bx, t_hbm, fy_hbm, fx_hbm, scaled_hbm, end_hbm,
           fields, ping, fy, fx, final, scaled, stats, gathered,
           load_sem, send_sem, recv_sem, stat_send, stat_recv, store_sem):
    row, col = lax.axis_index("rows"), lax.axis_index("cols")
    top = max(DEPTHS)

    def exists(dy, dx):
        ok = None
        for step, here, count in ((dy, row, rows), (dx, col, cols)):
            if step:
                inside = (here > 0) if step < 0 else (here < count - 1)
                ok = inside if ok is None else jnp.logical_and(ok, inside)
        return ok

    loads = [
        pltpu.make_async_copy(t_hbm, fields.at[0, pl.ds(top, by), pl.ds(PAD, bx)], load_sem.at[0]),
        pltpu.make_async_copy(fy_hbm, fy.at[pl.ds(top, by), pl.ds(PAD, bx)], load_sem.at[1]),
        pltpu.make_async_copy(fx_hbm, fx.at[pl.ds(top, by), pl.ds(PAD, bx)], load_sem.at[2]),
    ]
    for load in loads:
        load.start()

    barrier = pltpu.get_barrier_semaphore()

    @pl.loop(1, cols)
    def _(k):
        pl.semaphore_signal(barrier, inc=1, device_id={"cols": lax.rem(col + k, cols)}, device_id_type=MESH)

    for dy, dx in SIDES:
        if dy:
            @pl.when(exists(dy, dx))
            def _():
                pl.semaphore_signal(barrier, inc=1, device_id={"rows": row + dy, "cols": col + dx},
                                    device_id_type=MESH)

    width = bx + 2 * PAD
    for dy in (-1, 1):
        lines = pl.ds(0, top) if dy < 0 else pl.ds(top + by, top)

        @pl.when(jnp.logical_not(exists(dy, 0)))
        def _():
            blank = jnp.zeros((top, width, 128), jnp.float32)
            for e in range(len(DEPTHS)):
                fields[e, lines] = blank
            for b in range(2):
                ping[b, lines] = blank
            fy[lines] = blank
            fx[lines] = blank
    for dx in (-1, 1):
        strip = pl.ds(0, PAD) if dx < 0 else pl.ds(PAD + bx, PAD)

        @pl.when(jnp.logical_not(exists(0, dx)))
        def _():
            @pl.loop(0, by + 2 * top)
            def _(y):
                blank = jnp.zeros((PAD, 128), jnp.float32)
                for e in range(len(DEPTHS)):
                    fields[e, y, strip] = blank
                fy[y, strip] = blank
                fx[y, strip] = blank

    def one(n, count):
        return (n + count - 1) // count

    upright = one(row, rows) + one(rows - 1 - row, rows)
    across = one(col, cols) + one(cols - 1 - col, cols)
    pl.semaphore_wait(barrier, cols - 1 + upright * (1 + across))

    def copies(e, side):
        dy, dx = SIDES[side]
        target = {"rows": row + dy, "cols": col + dx}
        corner = 1 if dy and dx else 0
        out = []
        depth = DEPTHS[e]
        jobs = [(t_hbm if e == 0 else None, fields.at[e], depth - corner)]
        if e == 0:
            jobs += [(fy_hbm, fy, top - 1 - corner), (fx_hbm, fx, top - 1 - corner)]
        for i, (src, dst, d) in enumerate(jobs):
            if d <= 0:
                continue
            ys, yd = spans(dy, d, by, top)
            xs, xd = spans(dx, d, bx, PAD)
            if src is None:
                src = fields.at[e, pl.ds(top, by), pl.ds(PAD, bx)]
            out.append(pltpu.make_async_remote_copy(
                src_ref=src.at[ys, xs], dst_ref=dst.at[yd, xd],
                send_sem=send_sem.at[e, side, i], recv_sem=recv_sem.at[e, side, i],
                device_id=target, device_id_type=MESH))
        return out

    def start(e):
        for i in range(3):
            for side, (dy, dx) in enumerate(SIDES):
                mine = copies(e, side)
                if i < len(mine):
                    @pl.when(exists(dy, dx))
                    def _():
                        mine[i].start()

    def finish(e):
        for side, (dy, dx) in enumerate(SIDES):
            @pl.when(exists(-dy, -dx))
            def _():
                for copy in copies(e, side):
                    copy.wait_recv()

    def drain(e):
        for side, (dy, dx) in enumerate(SIDES):
            @pl.when(exists(dy, dx))
            def _():
                for copy in copies(e, side):
                    copy.wait_send()

    column = lax.broadcasted_iota(jnp.int32, (1, width, 128), 1)
    keep = jnp.logical_and(
        jnp.logical_or(column >= PAD, jnp.broadcast_to(col > 0, column.shape)),
        jnp.logical_or(column < PAD + bx, jnp.broadcast_to(col < cols - 1, column.shape)))

    def update(src, y, k):
        c = src[pl.ds(y, k)]
        above, below = src[pl.ds(y + 1, k)], src[pl.ds(y - 1, k)]
        right, left = pltpu.roll(c, width - 1, 1), pltpu.roll(c, 1, 1)
        spread = (above + below) + (right + left)
        return (0.8 * c + 0.05 * spread) - fy[pl.ds(y, k)] * (above - below) - fx[pl.ds(y, k)] * (right - left)

    def advance(src, dst, margin):
        k = 2

        @pl.loop(0, by // k)
        def _(i):
            y = top + i * k
            dst[pl.ds(y, k)] = jnp.where(keep, update(src, y, k), 0.0)
        for dy in (-1, 1):
            @pl.when(exists(dy, 0))
            def _():
                y = top - margin if dy < 0 else top + by
                for j in range(margin):
                    dst[pl.ds(y + j, 1)] = jnp.where(keep, update(src, y + j, 1), 0.0)

    def advance_last(src, write):
        k = 2

        @pl.loop(0, by // k)
        def _(i):
            y = top + i * k
            write(i * k, k, update(src, y, k)[:, PAD:PAD + bx])

    start(0)
    for load in loads:
        load.wait()
    for e, depth in enumerate(DEPTHS):
        finish(e)
        src = fields.at[e]
        for s in range(depth - 1):
            dst = ping.at[s % 2]
            advance(src, dst, depth - 1 - s)
            src = dst
        if e + 1 < len(DEPTHS):
            def write(y, k, new):
                fields[e + 1, pl.ds(top + y, k), pl.ds(PAD, bx)] = new
            advance_last(src, write)
            start(e + 1)
        else:
            def write(y, k, new):
                final[pl.ds(y, k)] = new
            advance_last(src, write)

    end_copy = pltpu.make_async_copy(final, end_hbm, store_sem.at[0])
    end_copy.start()

    g = 8

    @pl.loop(0, by // g)
    def _(i):
        block = final[pl.ds(i * g, g)]
        mean = jnp.sum(block, axis=1) / bx
        off = block - mean[:, None, :]
        stats[0, pl.ds(i * g, g)] = mean
        stats[1, pl.ds(i * g, g)] = jnp.sum(off * off, axis=1)

    def share(k):
        return pltpu.make_async_remote_copy(
            src_ref=stats, dst_ref=gathered.at[k - 1],
            send_sem=stat_send.at[k - 1], recv_sem=stat_recv.at[k - 1],
            device_id={"cols": lax.rem(col + k, cols)}, device_id_type=MESH)

    @pl.loop(1, cols)
    def _(k):
        share(k).start()

    @pl.loop(1, cols)
    def _(k):
        share(k).wait_recv()

    @pl.loop(0, by // g)
    def _(i):
        lines = pl.ds(i * g, g)
        mean0 = stats[0, lines]
        mean = lax.fori_loop(0, cols - 1, lambda j, s: s + gathered[j, 0, lines], mean0) / cols
        d0 = mean0 - mean

        def add(j, s):
            d = gathered[j, 0, lines] - mean
            return s + (gathered[j, 1, lines] + bx * (d * d))
        spread = lax.fori_loop(0, cols - 1, add, stats[1, lines] + bx * (d0 * d0))
        scale = lax.rsqrt(spread / (bx * cols) + 0.0001)
        scaled[lines] = (final[lines] - mean[:, None, :]) * scale[:, None, :]

    scaled_copy = pltpu.make_async_copy(scaled, scaled_hbm, store_sem.at[1])
    scaled_copy.start()
    for e in range(len(DEPTHS)):
        drain(e)

    @pl.loop(1, cols)
    def _(k):
        share(k).wait_send()
    end_copy.wait()
    scaled_copy.wait()


def shards(rows, cols, tracer, flow_y, flow_x):
    by, bx, species = tracer.shape
    top = max(DEPTHS)
    exchanges = len(DEPTHS)
    padded = (by + 2 * top, bx + 2 * PAD, species)
    block = jax.ShapeDtypeStruct(tracer.shape, jnp.float32)
    hbm = pl.BlockSpec(memory_space=pl.ANY)
    return pl.pallas_call(
        functools.partial(kernel, rows, cols, by, bx),
        out_shape=(block, block),
        in_specs=[hbm] * 3,
        out_specs=(hbm, hbm),
        scratch_shapes=[
            pltpu.VMEM((exchanges,) + padded, jnp.float32),
            pltpu.VMEM((2,) + padded, jnp.float32),
            pltpu.VMEM(padded, jnp.float32),
            pltpu.VMEM(padded, jnp.float32),
            pltpu.VMEM(tracer.shape, jnp.float32),
            pltpu.VMEM(tracer.shape, jnp.float32),
            pltpu.VMEM((2, by, species), jnp.float32),
            pltpu.VMEM((cols - 1, 2, by, species), jnp.float32),
            pltpu.SemaphoreType.DMA((3,)),
            pltpu.SemaphoreType.DMA((exchanges, 8, 3)),
            pltpu.SemaphoreType.DMA((exchanges, 8, 3)),
            pltpu.SemaphoreType.DMA((cols - 1,)),
            pltpu.SemaphoreType.DMA((cols - 1,)),
            pltpu.SemaphoreType.DMA((2,)),
        ],
        compiler_params=pltpu.CompilerParams(
            collective_id=0, has_side_effects=True, vmem_limit_bytes=40 * 1024 * 1024),
    )(tracer, flow_y, flow_x)


def solution(mesh):
    placed = P(("site", "rows"), "cols", None)
    return jax.shard_map(
        functools.partial(shards, mesh.shape["rows"], mesh.shape["cols"]),
        mesh=mesh,
        in_specs=(placed,) * 3,
        out_specs=(placed, placed),
        check_vma=False,
    )
```

time: 119 us -> 31.8 us (0.27)
  blocking collectives: 69.4 us -> 0 us
  Pallas kernels: 0 us -> 26.2 us
  starting transfers between devices: 22 us -> 0 us
  waiting for transfers between devices: 17.7 us -> 0 us
  other arithmetic: 5.2 us -> 0 us
  local copies, waits for them, and re-layouts: 2.94 us -> 4.71 us
    psum x2 -> x0, blocking collectives: 69.4 us -> none  [the longest x1 36.4 us: shards(): line_mean = lax.psum(jnp.sum(tracer, axis=1, keepdims=True), 'cols') / count]
    pallas_call x0 -> x1, Pallas kernels: none -> 26.2 us  [shards(): pl.pallas_call(functools.partial(kernel, rows, cols, by, bx), out_shape=(...]
    ppermute x8 -> x0, starting transfers between devices: 22 us -> none  [the longest x4 16.9 us: with_halo(): lax.ppermute(lax.slice_in_dim(block, block.shape[dim] - width, None, axis...]
    ppermute x8 -> x0, waiting for transfers between devices: 17.7 us -> none  [the longest x4 15.5 us: with_halo(): lax.ppermute(lax.slice_in_dim(block, block.shape[dim] - width, None, axis...]
    select_n x5 -> x0, other arithmetic: 3.2 us -> none  [shards(): values = jnp.where(keep_cells.reshape((-1,) + (1,) * 1), values, 0.0)]
    unnamed x11 -> x8, local copies, waits for them, and re-layouts: 1.78 us -> 4.71 us
  transfers between devices with their start and end apart: 8 -> 0, of which waited for: 4 -> 0; matrix products, arithmetic and copies ran while one was open for 0% -> 0% of each run, Pallas kernels for 0% -> 0%
where the time goes in v1:
time: 31.8 us; the launch traced here: 31.5 us
  Pallas kernels  26.2 us (82%)
  local copies, waits for them, and re-layouts  4.71 us (15%)
  between operations  0.65 us (2%)
    pallas_call x1, Pallas kernels, shards(): pl.pallas_call(functools.partial(kernel, rows, cols, by, bx), out_shape=(...  26.2 us
    unnamed x8, local copies, waits for them, and re-layouts  4.71 us

profile of v1, /device:TPU:0, one launch (start us, length us, event | category | flops | bytes accessed | tf_op | source)
XLA Modules:
  0.0 31.5 jit_solution(11649436063233677244)
XLA Ops:
  0.6 0.0 copy-start
  0.6 1.0 %copy-done = f32[32,32,128]{2,1,0:T(8,128)S(1)} copy-done((f32[32,32,128]{2,1,0:T(8,128)S(1)}, f32[32,32,128]{2,1,0:T(8,128)}, u32[]{:S(2)}) %copy-start) | copy-done | bytes 524312
  1.7 0.0 copy-start.1
  1.7 1.0 %copy-done.1 = f32[32,32,128]{2,1,0:T(8,128)S(1)} copy-done((f32[32,32,128]{2,1,0:T(8,128)S(1)}, f32[32,32,128]{2,1,0:T(8,128)}, u32[]{:S(2)}) %copy-start.1) | copy-done | bytes 524312
  2.7 0.0 copy-start.2
  2.7 1.0 %copy-done.2 = f32[32,32,128]{2,1,0:T(8,128)S(1)} copy-done((f32[32,32,128]{2,1,0:T(8,128)S(1)}, f32[32,32,128]{2,1,0:T(8,128)}, u32[]{:S(2)}) %copy-start.2) | copy-done | bytes 524312
  3.8 26.2 %shard_map.50 = (f32[32,32,128]{2,1,0:T(8,128)S(1)}, f32[32,32,128]{2,1,0:T(8,128)S(1)}) custom-call(f32[32,32,128]{2,1,0:T(8,128)S(1)} %copy-done, f32[32,32,128]{2,1,0:T(8,128)S(1)} %copy-done.1, f32[32,32,128]{2,1,0:T(8,128)S(1)} %copy-done.2), custom_call_target="tpu_custom_call" | custom-call | tf_op jit(solution)/shard_map/pallas_call | solution.py:251
  29.9 0.8 %copy.7 = f32[32,32,128]{2,1,0:T(8,128)} copy(f32[32,32,128]{2,1,0:T(8,128)S(1)} %get-tuple-element.4) | data formatting | bytes 1048576
  30.7 0.8 %copy.8 = f32[32,32,128]{2,1,0:T(8,128)} copy(f32[32,32,128]{2,1,0:T(8,128)S(1)} %get-tuple-element.5) | data formatting | bytes 1048576
Async XLA Ops:
  0.6 1.0 %copy-start = (f32[32,32,128]{2,1,0:T(8,128)S(1)}, f32[32,32,128]{2,1,0:T(8,128)}, u32[]{:S(2)}) copy-start(f32[32,32,128]{2,1,0:T(8,128)} %t_hbm.1) | copy-start | bytes 1572868
  1.7 1.0 %copy-start.1 = (f32[32,32,128]{2,1,0:T(8,128)S(1)}, f32[32,32,128]{2,1,0:T(8,128)}, u32[]{:S(2)}) copy-start(f32[32,32,128]{2,1,0:T(8,128)} %fy_hbm.1) | copy-start | bytes 1572868
  2.7 1.0 %copy-start.2 = (f32[32,32,128]{2,1,0:T(8,128)S(1)}, f32[32,32,128]{2,1,0:T(8,128)}, u32[]{:S(2)}) copy-start(f32[32,32,128]{2,1,0:T(8,128)} %fx_hbm.1) | copy-start | bytes 1572868

commit v2 on v1

--- a/solution.py
+++ b/solution.py
@@ -13,16 +13,16 @@
 SIDES = tuple((dy, dx) for dy in (-1, 0, 1) for dx in (-1, 0, 1) if (dy, dx) != (0, 0))
 
 
-def spans(side, depth, size, first):
+def spans(side, depth, size, first, low):
     if side == 0:
         return pl.ds(0, size), pl.ds(first, size)
     if side < 0:
         return pl.ds(0, depth), pl.ds(first + size, depth)
-    return pl.ds(size - depth, depth), pl.ds(first - depth, depth)
-
-
-def kernel(rows, cols, by, bx, t_hbm, fy_hbm, fx_hbm, scaled_hbm, end_hbm,
-           fields, ping, fy, fx, final, scaled, stats, gathered,
+    return pl.ds(size - depth, depth), pl.ds(low - depth, depth)
+
+
+def kernel(rows, cols, by, bx, t_hbm, fy_hbm, fx_hbm, end_hbm, lines_hbm,
+           fields, ping, fy, fx, final, moments, stats, gathered,
            load_sem, send_sem, recv_sem, stat_send, stat_recv, store_sem):
     row, col = lax.axis_index("rows"), lax.axis_index("cols")
     top = max(DEPTHS)
@@ -36,9 +36,9 @@
         return ok
 
     loads = [
-        pltpu.make_async_copy(t_hbm, fields.at[0, pl.ds(top, by), pl.ds(PAD, bx)], load_sem.at[0]),
-        pltpu.make_async_copy(fy_hbm, fy.at[pl.ds(top, by), pl.ds(PAD, bx)], load_sem.at[1]),
-        pltpu.make_async_copy(fx_hbm, fx.at[pl.ds(top, by), pl.ds(PAD, bx)], load_sem.at[2]),
+        pltpu.make_async_copy(t_hbm, fields.at[0, pl.ds(top, by), pl.ds(0, bx)], load_sem.at[0]),
+        pltpu.make_async_copy(fy_hbm, fy.at[pl.ds(top, by), pl.ds(0, bx)], load_sem.at[1]),
+        pltpu.make_async_copy(fx_hbm, fx.at[pl.ds(top, by), pl.ds(0, bx)], load_sem.at[2]),
     ]
     for load in loads:
         load.start()
@@ -56,7 +56,7 @@
                 pl.semaphore_signal(barrier, inc=1, device_id={"rows": row + dy, "cols": col + dx},
                                     device_id_type=MESH)
 
-    width = bx + 2 * PAD
+    width = bx + PAD
     for dy in (-1, 1):
         lines = pl.ds(0, top) if dy < 0 else pl.ds(top + by, top)
 
@@ -70,13 +70,13 @@
             fy[lines] = blank
             fx[lines] = blank
     for dx in (-1, 1):
-        strip = pl.ds(0, PAD) if dx < 0 else pl.ds(PAD + bx, PAD)
+        strip = pl.ds(width - PAD // 2, PAD // 2) if dx < 0 else pl.ds(bx, PAD // 2)
 
         @pl.when(jnp.logical_not(exists(0, dx)))
         def _():
             @pl.loop(0, by + 2 * top)
             def _(y):
-                blank = jnp.zeros((PAD, 128), jnp.float32)
+                blank = jnp.zeros((PAD // 2, 128), jnp.float32)
                 for e in range(len(DEPTHS)):
                     fields[e, y, strip] = blank
                 fy[y, strip] = blank
@@ -101,10 +101,10 @@
         for i, (src, dst, d) in enumerate(jobs):
             if d <= 0:
                 continue
-            ys, yd = spans(dy, d, by, top)
-            xs, xd = spans(dx, d, bx, PAD)
+            ys, yd = spans(dy, d, by, top, top)
+            xs, xd = spans(dx, d, bx, 0, width)
             if src is None:
-                src = fields.at[e, pl.ds(top, by), pl.ds(PAD, bx)]
+                src = fields.at[e, pl.ds(top, by), pl.ds(0, bx)]
             out.append(pltpu.make_async_remote_copy(
                 src_ref=src.at[ys, xs], dst_ref=dst.at[yd, xd],
                 send_sem=send_sem.at[e, side, i], recv_sem=recv_sem.at[e, side, i],
@@ -136,8 +136,9 @@
 
     column = lax.broadcasted_iota(jnp.int32, (1, width, 128), 1)
     keep = jnp.logical_and(
-        jnp.logical_or(column >= PAD, jnp.broadcast_to(col > 0, column.shape)),
-        jnp.logical_or(column < PAD + bx, jnp.broadcast_to(col < cols - 1, column.shape)))
+        jnp.logical_or(column < bx + PAD // 2, jnp.broadcast_to(col > 0, column.shape)),
+        jnp.logical_or(jnp.logical_or(column < bx, column >= bx + PAD // 2),
+                       jnp.broadcast_to(col < cols - 1, column.shape)))
 
     def update(src, y, k):
         c = src[pl.ds(y, k)]
@@ -147,7 +148,7 @@
         return (0.8 * c + 0.05 * spread) - fy[pl.ds(y, k)] * (above - below) - fx[pl.ds(y, k)] * (right - left)
 
     def advance(src, dst, margin):
-        k = 2
+        k = 8
 
         @pl.loop(0, by // k)
         def _(i):
@@ -161,12 +162,12 @@
                     dst[pl.ds(y + j, 1)] = jnp.where(keep, update(src, y + j, 1), 0.0)
 
     def advance_last(src, write):
-        k = 2
+        k = 8
 
         @pl.loop(0, by // k)
         def _(i):
             y = top + i * k
-            write(i * k, k, update(src, y, k)[:, PAD:PAD + bx])
+            write(i * k, k, update(src, y, k)[:, :bx])
 
     start(0)
     for load in loads:
@@ -180,7 +181,7 @@
             src = dst
         if e + 1 < len(DEPTHS):
             def write(y, k, new):
-                fields[e + 1, pl.ds(top + y, k), pl.ds(PAD, bx)] = new
+                fields[e + 1, pl.ds(top + y, k), pl.ds(0, bx)] = new
             advance_last(src, write)
             start(e + 1)
         else:
@@ -226,11 +227,11 @@
             d = gathered[j, 0, lines] - mean
             return s + (gathered[j, 1, lines] + bx * (d * d))
         spread = lax.fori_loop(0, cols - 1, add, stats[1, lines] + bx * (d0 * d0))
-        scale = lax.rsqrt(spread / (bx * cols) + 0.0001)
-        scaled[lines] = (final[lines] - mean[:, None, :]) * scale[:, None, :]
-
-    scaled_copy = pltpu.make_async_copy(scaled, scaled_hbm, store_sem.at[1])
-    scaled_copy.start()
+        moments[0, lines] = mean
+        moments[1, lines] = lax.rsqrt(spread / (bx * cols) + 0.0001)
+
+    lines_copy = pltpu.make_async_copy(moments, lines_hbm, store_sem.at[1])
+    lines_copy.start()
     for e in range(len(DEPTHS)):
         drain(e)
 
@@ -238,19 +239,47 @@
     def _(k):
         share(k).wait_send()
     end_copy.wait()
-    scaled_copy.wait()
+    lines_copy.wait()
+
+
+def scale_kernel(end_hbm, lines_hbm, scaled_out, end_out, end, lines, scaled, sem):
+    by = end.shape[0]
+    parts = 4
+    g = by // parts
+
+    def part(i):
+        return pl.ds(i * g, g)
+
+    head = pltpu.make_async_copy(lines_hbm, lines, sem.at[0, 0])
+    head.start()
+    loads = [pltpu.make_async_copy(end_hbm.at[part(i)], end.at[part(i)], sem.at[1, i]) for i in range(parts)]
+    for load in loads:
+        load.start()
+    head.wait()
+    stores = []
+    for i in range(parts):
+        loads[i].wait()
+        store = pltpu.make_async_copy(end.at[part(i)], end_out.at[part(i)], sem.at[2, i])
+        store.start()
+        stores.append(store)
+        scaled[part(i)] = (end[part(i)] - lines[0, part(i)][:, None, :]) * lines[1, part(i)][:, None, :]
+        store = pltpu.make_async_copy(scaled.at[part(i)], scaled_out.at[part(i)], sem.at[3, i])
+        store.start()
+        stores.append(store)
+    for store in stores:
+        store.wait()
 
 
 def shards(rows, cols, tracer, flow_y, flow_x):
     by, bx, species = tracer.shape
     top = max(DEPTHS)
     exchanges = len(DEPTHS)
-    padded = (by + 2 * top, bx + 2 * PAD, species)
+    padded = (by + 2 * top, bx + PAD, species)
     block = jax.ShapeDtypeStruct(tracer.shape, jnp.float32)
     hbm = pl.BlockSpec(memory_space=pl.ANY)
-    return pl.pallas_call(
+    end, lines = pl.pallas_call(
         functools.partial(kernel, rows, cols, by, bx),
-        out_shape=(block, block),
+        out_shape=(block, jax.ShapeDtypeStruct((2, by, species), jnp.float32)),
         in_specs=[hbm] * 3,
         out_specs=(hbm, hbm),
         scratch_shapes=[
@@ -259,7 +288,7 @@
             pltpu.VMEM(padded, jnp.float32),
             pltpu.VMEM(padded, jnp.float32),
             pltpu.VMEM(tracer.shape, jnp.float32),
-            pltpu.VMEM(tracer.shape, jnp.float32),
+            pltpu.VMEM((2, by, species), jnp.float32),
             pltpu.VMEM((2, by, species), jnp.float32),
             pltpu.VMEM((cols - 1, 2, by, species), jnp.float32),
             pltpu.SemaphoreType.DMA((3,)),
@@ -270,8 +299,21 @@
             pltpu.SemaphoreType.DMA((2,)),
         ],
         compiler_params=pltpu.CompilerParams(
-            collective_id=0, has_side_effects=True, vmem_limit_bytes=40 * 1024 * 1024),
+            collective_id=0, has_side_effects=True, vmem_limit_bytes=67043328),
     )(tracer, flow_y, flow_x)
+    return pl.pallas_call(
+        scale_kernel,
+        out_shape=(block, block),
+        in_specs=[hbm] * 2,
+        out_specs=(hbm, hbm),
+        scratch_shapes=[
+            pltpu.VMEM(tracer.shape, jnp.float32),
+            pltpu.VMEM((2, by, species), jnp.float32),
+            pltpu.VMEM(tracer.shape, jnp.float32),
+            pltpu.SemaphoreType.DMA((4, 4)),
+        ],
+        compiler_params=pltpu.CompilerParams(vmem_limit_bytes=67043328),
+    )(end, lines)
 
 
 def solution(mesh):

time: 31.8 us -> 28.8 us (0.906)
  local copies, waits for them, and re-layouts: 4.71 us -> 0 us
  Pallas kernels: 26.2 us -> 28 us
    unnamed x8 -> x0, local copies, waits for them, and re-layouts: 4.71 us -> none
    pallas_call x0 -> x1, Pallas kernels: none -> 2.02 us  [shards(): pl.pallas_call(scale_kernel, out_shape=(block, block), in_specs=[hbm] * 2...]
where the time goes in v2:
time: 28.8 us; the launch traced here: 28.6 us
  Pallas kernels  28 us (97%)
  between operations  0.64 us (2%)
    pallas_call x1, Pallas kernels, shards(): pl.pallas_call(functools.partial(kernel, rows, cols, by, bx), out_shape=(...  26 us
    pallas_call x1, Pallas kernels, shards(): pl.pallas_call(scale_kernel, out_shape=(block, block), in_specs=[hbm] * 2...  2.02 us

profile of v2, /device:TPU:0, one launch (start us, length us, event | category | flops | bytes accessed | tf_op | source)
XLA Modules:
  0.0 28.6 jit_solution(6812503089128700282)
XLA Ops:
  0.6 26.0 %shard_map.50 = (f32[32,32,128]{2,1,0:T(8,128)}, f32[2,32,128]{2,1,0:T(8,128)}) custom-call(f32[32,32,128]{2,1,0:T(8,128)} %t_hbm.1, f32[32,32,128]{2,1,0:T(8,128)} %fy_hbm.1, f32[32,32,128]{2,1,0:T(8,128)} %fx_hbm.1), custom_call_target="tpu_custom_call" | custom-call | tf_op jit(solution)/shard_map/pallas_call | solution.py:280
  26.6 2.0 %shard_map.51 = (f32[32,32,128]{2,1,0:T(8,128)}, f32[32,32,128]{2,1,0:T(8,128)}) custom-call(f32[32,32,128]{2,1,0:T(8,128)} %get-tuple-element.4.end_hbm, f32[2,32,128]{2,1,0:T(8,128)} %get-tuple-element.5.lines_hbm), custom_call_target="tpu_custom_call" | custom-call | tf_op jit(solution)/shard_map/pallas_call | solution.py:304

commit v3 on v2

--- a/solution.py
+++ b/solution.py
@@ -21,9 +21,9 @@
     return pl.ds(size - depth, depth), pl.ds(low - depth, depth)
 
 
-def kernel(rows, cols, by, bx, t_hbm, fy_hbm, fx_hbm, end_hbm, lines_hbm,
-           fields, ping, fy, fx, final, moments, stats, gathered,
-           load_sem, send_sem, recv_sem, stat_send, stat_recv, store_sem):
+def kernel(rows, cols, by, bx, t_hbm, fy_hbm, fx_hbm, final, moments,
+           fields, ping, fy, fx, stats, gathered,
+           load_sem, send_sem, recv_sem, stat_send, stat_recv):
     row, col = lax.axis_index("rows"), lax.axis_index("cols")
     top = max(DEPTHS)
 
@@ -189,9 +189,6 @@
                 final[pl.ds(y, k)] = new
             advance_last(src, write)
 
-    end_copy = pltpu.make_async_copy(final, end_hbm, store_sem.at[0])
-    end_copy.start()
-
     g = 8
 
     @pl.loop(0, by // g)
@@ -229,43 +226,27 @@
         spread = lax.fori_loop(0, cols - 1, add, stats[1, lines] + bx * (d0 * d0))
         moments[0, lines] = mean
         moments[1, lines] = lax.rsqrt(spread / (bx * cols) + 0.0001)
-
-    lines_copy = pltpu.make_async_copy(moments, lines_hbm, store_sem.at[1])
-    lines_copy.start()
     for e in range(len(DEPTHS)):
         drain(e)
 
     @pl.loop(1, cols)
     def _(k):
         share(k).wait_send()
-    end_copy.wait()
-    lines_copy.wait()
-
-
-def scale_kernel(end_hbm, lines_hbm, scaled_out, end_out, end, lines, scaled, sem):
-    by = end.shape[0]
+
+
+def scale_kernel(end, lines, scaled_out, end_out, scaled, sem):
     parts = 4
-    g = by // parts
-
-    def part(i):
-        return pl.ds(i * g, g)
-
-    head = pltpu.make_async_copy(lines_hbm, lines, sem.at[0, 0])
-    head.start()
-    loads = [pltpu.make_async_copy(end_hbm.at[part(i)], end.at[part(i)], sem.at[1, i]) for i in range(parts)]
-    for load in loads:
-        load.start()
-    head.wait()
-    stores = []
+    g = end.shape[0] // parts
+    whole = pltpu.make_async_copy(end, end_out, sem.at[parts])
+    stores = [whole]
     for i in range(parts):
-        loads[i].wait()
-        store = pltpu.make_async_copy(end.at[part(i)], end_out.at[part(i)], sem.at[2, i])
+        part = pl.ds(i * g, g)
+        scaled[part] = (end[part] - lines[0, part][:, None, :]) * lines[1, part][:, None, :]
+        store = pltpu.make_async_copy(scaled.at[part], scaled_out.at[part], sem.at[i])
         store.start()
         stores.append(store)
-        scaled[part(i)] = (end[part(i)] - lines[0, part(i)][:, None, :]) * lines[1, part(i)][:, None, :]
-        store = pltpu.make_async_copy(scaled.at[part(i)], scaled_out.at[part(i)], sem.at[3, i])
-        store.start()
-        stores.append(store)
+        if i == 0:
+            whole.start()
     for store in stores:
         store.wait()
 
@@ -279,16 +260,14 @@
     hbm = pl.BlockSpec(memory_space=pl.ANY)
     end, lines = pl.pallas_call(
         functools.partial(kernel, rows, cols, by, bx),
-        out_shape=(block, jax.ShapeDtypeStruct((2, by, species), jnp.float32)),
-        in_specs=[hbm] * 3,
-        out_specs=(hbm, hbm),
+        out_shape=(pltpu.VMEM(tracer.shape, jnp.float32), pltpu.VMEM((2, by, species), jnp.float32)),
+        in_specs=[pl.BlockSpec(memory_space=pltpu.HBM)] * 3,
+        out_specs=(pl.BlockSpec(memory_space=pltpu.VMEM),) * 2,
         scratch_shapes=[
             pltpu.VMEM((exchanges,) + padded, jnp.float32),
             pltpu.VMEM((2,) + padded, jnp.float32),
             pltpu.VMEM(padded, jnp.float32),
             pltpu.VMEM(padded, jnp.float32),
-            pltpu.VMEM(tracer.shape, jnp.float32),
-            pltpu.VMEM((2, by, species), jnp.float32),
             pltpu.VMEM((2, by, species), jnp.float32),
             pltpu.VMEM((cols - 1, 2, by, species), jnp.float32),
             pltpu.SemaphoreType.DMA((3,)),
@@ -296,23 +275,20 @@
             pltpu.SemaphoreType.DMA((exchanges, 8, 3)),
             pltpu.SemaphoreType.DMA((cols - 1,)),
             pltpu.SemaphoreType.DMA((cols - 1,)),
-            pltpu.SemaphoreType.DMA((2,)),
         ],
         compiler_params=pltpu.CompilerParams(
-            collective_id=0, has_side_effects=True, vmem_limit_bytes=67043328),
+            collective_id=0, has_side_effects=True, vmem_limit_bytes=67043328 - 1024 * 1024),
     )(tracer, flow_y, flow_x)
     return pl.pallas_call(
         scale_kernel,
         out_shape=(block, block),
-        in_specs=[hbm] * 2,
+        in_specs=[pl.BlockSpec(memory_space=pltpu.VMEM)] * 2,
         out_specs=(hbm, hbm),
         scratch_shapes=[
             pltpu.VMEM(tracer.shape, jnp.float32),
-            pltpu.VMEM((2, by, species), jnp.float32),
-            pltpu.VMEM(tracer.shape, jnp.float32),
-            pltpu.SemaphoreType.DMA((4, 4)),
+            pltpu.SemaphoreType.DMA((5,)),
         ],
-        compiler_params=pltpu.CompilerParams(vmem_limit_bytes=67043328),
+        compiler_params=pltpu.CompilerParams(vmem_limit_bytes=40 * 1024 * 1024),
     )(end, lines)
 
 

time: 28.8 us -> 27.2 us (0.944)
  Pallas kernels: 28 us -> 26.4 us
    pallas_call x1, Pallas kernels: 2.02 us -> 1.02 us  [shards(): pl.pallas_call(scale_kernel, out_shape=(block, block), in_specs=[pl.Block...]
    pallas_call x1, Pallas kernels: 26 us -> 25.4 us  [shards(): pl.pallas_call(functools.partial(kernel, rows, cols, by, bx), out_shape=(...]
where the time goes in v3:
time: 27.2 us; the launch traced here: 27.1 us
  Pallas kernels  26.4 us (97%)
  between operations  0.64 us (2%)
    pallas_call x1, Pallas kernels, shards(): pl.pallas_call(functools.partial(kernel, rows, cols, by, bx), out_shape=(...  25.4 us
    pallas_call x1, Pallas kernels, shards(): pl.pallas_call(scale_kernel, out_shape=(block, block), in_specs=[pl.Block...  1.02 us

profile of v3, /device:TPU:0, one launch (start us, length us, event | category | flops | bytes accessed | tf_op | source)
XLA Modules:
  0.0 27.1 jit_solution(14449004278490819242)
XLA Ops:
  0.6 25.4 %shard_map.50 = (f32[32,32,128]{2,1,0:T(8,128)S(1)}, f32[2,32,128]{2,1,0:T(8,128)S(1)}) custom-call(f32[32,32,128]{2,1,0:T(8,128)} %t_hbm.1, f32[32,32,128]{2,1,0:T(8,128)} %fy_hbm.1, f32[32,32,128]{2,1,0:T(8,128)} %fx_hbm.1), custom_call_target="tpu_custom_call" | custom-call | tf_op jit(solution)/shard_map/pallas_call | solution.py:261
  26.0 1.0 %shard_map.51 = (f32[32,32,128]{2,1,0:T(8,128)}, f32[32,32,128]{2,1,0:T(8,128)}) custom-call(f32[32,32,128]{2,1,0:T(8,128)S(1)} %get-tuple-element.4.end, f32[2,32,128]{2,1,0:T(8,128)S(1)} %get-tuple-element.5.lines), custom_call_target="tpu_custom_call" | custom-call | tf_op jit(solution)/shard_map/pallas_call | solution.py:282

commit v4 on v3

--- a/solution.py
+++ b/solution.py
@@ -217,13 +217,10 @@
     def _(i):
         lines = pl.ds(i * g, g)
         mean0 = stats[0, lines]
-        mean = lax.fori_loop(0, cols - 1, lambda j, s: s + gathered[j, 0, lines], mean0) / cols
+        mean = (mean0 + jnp.sum(gathered[:, 0, lines], axis=0)) / cols
         d0 = mean0 - mean
-
-        def add(j, s):
-            d = gathered[j, 0, lines] - mean
-            return s + (gathered[j, 1, lines] + bx * (d * d))
-        spread = lax.fori_loop(0, cols - 1, add, stats[1, lines] + bx * (d0 * d0))
+        d = gathered[:, 0, lines] - mean
+        spread = stats[1, lines] + bx * (d0 * d0) + jnp.sum(gathered[:, 1, lines] + bx * (d * d), axis=0)
         moments[0, lines] = mean
         moments[1, lines] = lax.rsqrt(spread / (bx * cols) + 0.0001)
     for e in range(len(DEPTHS)):

time: 27.2 us -> 26.9 us (0.989)
  Pallas kernels: 26.4 us -> 26.1 us
    pallas_call x1, Pallas kernels: 25.4 us -> 25.1 us  [shards(): pl.pallas_call(functools.partial(kernel, rows, cols, by, bx), out_shape=(...]
where the time goes in v4:
time: 26.9 us; the launch traced here: 26.8 us
  Pallas kernels  26.1 us (97%)
  between operations  0.64 us (2%)
    pallas_call x1, Pallas kernels, shards(): pl.pallas_call(functools.partial(kernel, rows, cols, by, bx), out_shape=(...  25.1 us
    pallas_call x1, Pallas kernels, shards(): pl.pallas_call(scale_kernel, out_shape=(block, block), in_specs=[pl.Block...  1.02 us

profile of v4, /device:TPU:0, one launch (start us, length us, event | category | flops | bytes accessed | tf_op | source)
XLA Modules:
  0.0 26.8 jit_solution(2355714694622571506)
XLA Ops:
  0.6 25.1 %shard_map.50 = (f32[32,32,128]{2,1,0:T(8,128)S(1)}, f32[2,32,128]{2,1,0:T(8,128)S(1)}) custom-call(f32[32,32,128]{2,1,0:T(8,128)} %t_hbm.1, f32[32,32,128]{2,1,0:T(8,128)} %fy_hbm.1, f32[32,32,128]{2,1,0:T(8,128)} %fx_hbm.1), custom_call_target="tpu_custom_call" | custom-call | tf_op jit(solution)/shard_map/pallas_call | solution.py:258
  25.8 1.0 %shard_map.51 = (f32[32,32,128]{2,1,0:T(8,128)}, f32[32,32,128]{2,1,0:T(8,128)}) custom-call(f32[32,32,128]{2,1,0:T(8,128)S(1)} %get-tuple-element.4.end, f32[2,32,128]{2,1,0:T(8,128)S(1)} %get-tuple-element.5.lines), custom_call_target="tpu_custom_call" | custom-call | tf_op jit(solution)/shard_map/pallas_call | solution.py:279
